TPU v7x, 32 devices: a whole 2x2x4 slice. The times are simulated.
32 devices in a mesh: gx: 8 (over z, x), gy: 4 (over y, core).
Axes of the slice: x: 2, y: 2, z: 4, core: 2. Of those that a mesh axis runs over, the one named last changes fastest.
Arguments:
- parcel_props: float32 [16, 131072], P(None, ('gx', 'gy')), may hold values from -6 to 6
- size_class: int32 [131072], P(('gx', 'gy')), may hold values from 0 to 7
- dest_owner: int32 [131072, 1], P(('gx', 'gy')), may hold values from 0 to 31; in each aligned block of 4096 rows (0 to 4095, 4096 to 8191, ...) at most 512 rows name the same one
- dest_local: int32 [131072], P(('gx', 'gy')), may hold values from 0 to 4095
- class_table: float32 [8, 16], replicated, may hold values from 0.5 to 2
- gas_density: float32 [256, 512], P('gx', 'gy'), may hold values from 0.5 to 2
- gas_rest: float32 [4, 256, 512], P(None, 'gx', 'gy'), may hold values from -6 to 6
Outputs:
- new_density: float32 [256, 512], P('gx', 'gy')
- new_rest: float32 [4, 256, 512], P(None, 'gx', 'gy')
Inputs may be any that keep to these rules, and one draw needn't show every extreme that they name: `dest_owner`: among the parcels of one device, no owner device is named by more than 512 of them, a bound that some block reaches.
All inputs are finite; a program needn't handle non-finite values.
Results may differ from a plain program's by a relative error of at most 0.00015.
Values sent between devices are 32-bit elements; how exact they have to be, the bound alone decides.
No kernel may reach another device: no remote copies, remote signals or barrier semaphores. Data moves between devices by JAX's collectives and lax.ppermute only.
A program may use at most 64 MiB of HBM per device.

v0:
```python
import math

import jax
import jax.numpy as jnp
from jax import lax
from jax.sharding import PartitionSpec as P


def with_halo(shard, sides, width):
    for axis, dim in sides:
        devices, length = (lax.axis_size(axis), shard.shape[dim])
        up = [(i, (i + 1) % devices) for i in range(devices - 1)]
        down = [(j, i) for i, j in up]
        last = lax.slice_in_dim(shard, length - width, length, axis=dim)
        leading = lax.slice_in_dim(shard, 0, width, axis=dim)
        before = lax.ppermute(last, axis, up)
        after = lax.ppermute(leading, axis, down)
        shard = jnp.concatenate([before, shard, after], axis=dim)
    return shard


def sources_of(props, classes, gas, table):
    count = table.shape[0]
    picks = (classes[None, :] == jnp.arange(count, dtype=jnp.int32)[:, None]).astype(jnp.float32)
    coef = jnp.dot(
        table.T, picks, precision=lax.Precision.HIGHEST, preferred_element_type=jnp.float32
    )
    mass = jnp.exp(0.5 * props[0])
    density = gas[0]
    velocity = gas[1:4] / density
    theta = gas[4] / density
    slip = props[1:4] - velocity
    rate = coef[0] * jax.nn.softplus(props[4] - theta)
    evapor = mass * (1.0 - jnp.exp(-rate))
    dragged = 1.0 - jnp.exp(-coef[1] * jnp.sqrt(1.0 + jnp.sum(slip * slip, axis=0)))
    moment = evapor * coef[2:5] * props[1:4] + mass * dragged * slip
    energy = evapor * (props[4] + jnp.sum(coef[5:] * props[5:], axis=0))
    return jnp.concatenate([evapor[None], moment, energy[None]], axis=0)


def cell_hot(cells, first, width):
    return (cells[None, :] == (first + jnp.arange(width, dtype=jnp.int32))[:, None]).astype(
        jnp.float32
    )


def look_up(table, cells):
    total = table.shape[1]
    width = math.gcd(total, 512)

    def look_advance(index, gathered):
        first = (index * width).astype(jnp.int32)
        block = lax.dynamic_slice_in_dim(table, first, width, 1)
        return gathered + jnp.dot(
            block,
            cell_hot(cells, first, width),
            precision=lax.Precision.HIGHEST,
            preferred_element_type=jnp.float32,
        )

    return lax.fori_loop(
        0, total // width, look_advance, jnp.zeros((table.shape[0], cells.shape[0]), jnp.float32)
    )


def deposit_into(source, cells, total):
    width = math.gcd(total, 512)

    def deposit_advance(index, field):
        first = (index * width).astype(jnp.int32)
        block = lax.dot_general(
            source,
            cell_hot(cells, first, width),
            (((1,), (1,)), ((), ())),
            precision=lax.Precision.HIGHEST,
            preferred_element_type=jnp.float32,
        )
        return lax.dynamic_update_slice_in_dim(field, block, first, 1)

    return lax.fori_loop(
        0, total // width, deposit_advance, jnp.zeros((source.shape[0], total), jnp.float32)
    )


def per_device(
    parcel_props, size_class, dest_owner, dest_local, class_table, gas_density, gas_rest
):
    width_x = lax.axis_size("gx")
    width_y = lax.axis_size("gy")
    devices = width_x * width_y
    parcels = parcel_props.shape[1]
    slab_x, slab_y = gas_density.shape
    capacity = max(2, 4 * parcels // devices)
    slots = devices * capacity
    owner = dest_owner[:, 0]
    member = (owner[:, None] == jnp.arange(devices, dtype=jnp.int32)[None, :]).astype(jnp.int32)
    rank = jnp.sum(jnp.cumsum(member, axis=0) * member, axis=1) - 1
    slot = owner * capacity + rank
    gas_flat = jnp.concatenate([gas_density[None], gas_rest], axis=0).reshape(5, slab_x * slab_y)
    float_buf = jnp.zeros((parcel_props.shape[0], slots), jnp.float32).at[:, slot].set(parcel_props)
    int_buf = (
        jnp.full((2, slots), -1, jnp.int32).at[:, slot].set(jnp.stack([size_class, dest_local]))
    )
    got_floats, got_ints = (
        lax.all_to_all(
            lax.all_to_all(
                float_buf.reshape(-1, width_x, width_y, capacity),
                "gx",
                split_axis=1,
                concat_axis=1,
                tiled=True,
            ),
            "gy",
            split_axis=2,
            concat_axis=2,
            tiled=True,
        ),
        lax.all_to_all(
            lax.all_to_all(
                int_buf.reshape(2, width_x, width_y, capacity),
                "gx",
                split_axis=1,
                concat_axis=1,
                tiled=True,
            ),
            "gy",
            split_axis=2,
            concat_axis=2,
            tiled=True,
        ),
    )
    props_in = got_floats.reshape(parcel_props.shape[0], slots)
    ints_in = got_ints.reshape(2, slots)
    cells = ints_in[1]
    safe = jnp.maximum(cells, 0)
    source = sources_of(props_in, ints_in[0], look_up(gas_flat, safe), class_table)
    deposit = deposit_into(source, cells, slab_x * slab_y).reshape(5, slab_x, slab_y)
    padded = with_halo(deposit, (("gx", 1), ("gy", 2)), 1)
    beside = padded[:, 2:, 1:-1] + padded[:, :-2, 1:-1] + padded[:, 1:-1, 2:] + padded[:, 1:-1, :-2]
    smooth = 0.4 * deposit + 0.15 * beside
    return (gas_density + smooth[0], gas_rest + smooth[1:])


def solution(mesh):
    return jax.shard_map(
        per_device,
        mesh=mesh,
        in_specs=(
            P(None, ("gx", "gy")),
            P(("gx", "gy")),
            P(("gx", "gy"), None),
            P(("gx", "gy")),
            P(),
            P("gx", "gy"),
            P(None, "gx", "gy"),
        ),
        out_specs=(P("gx", "gy"), P(None, "gx", "gy")),
        check_vma=False,
    )
```

profile of v0, /device:TPU:6, one launch (start us, length us, event | category | flops | bytes accessed | tf_op | source)
XLA Modules:
  0.0 321.2 jit_solution(1331157601480989141)
XLA Ops:
  1.4 9.2 %reduce-window.6 = s32[32,32,128]{2,1,0:T(8,128)S(1)} reduce-window(s32[32,32,128]{2,1,0:T(8,128)S(1)} %fusion.26, s32[]{:T(128)} %constant.78.clone.1), window={size=1x1x128 pad=0_0x0_0x127_0}, to_apply=%region_0.0 | reduce-window | flops 16646144 | bytes 1048580 | tf_op jit(solution)/shard_map/reduce-window
  15.1 14.3 %scatter_custom_fusion = s32[2,16384]{0,1:T(8,128)} fusion(s32[4096]{0:T(1024)S(1)} %bitcast.88, s32[4096,2]{1,0:T(8,128)S(1)} %copy.15, s32[]{:T(128)} %constant.80.clone.1), kind=kCustom, calls=%fused_computation.20 | custom fusion | bytes 131076 | tf_op jit(solution)/shard_map/scatter | solution.py:102
  29.4 5.2 %copy.16 = s32[2,8,4,512]{3,2,0,1:T(4,128)S(1)} copy(s32[2,8,4,512]{0,3,2,1:T(8,128)} %bitcast.64) | data formatting | bytes 262144 | tf_op jit(solution)/shard_map/reshape | solution.py:120
  34.6 11.7 %all_to_all.20 = s32[2,8,4,512]{3,2,0,1:T(4,128)S(1)} all-to-all(s32[2,8,4,512]{3,2,0,1:T(4,128)S(1)} %copy.16), channel_id=1, replica_groups=mesh['gx'=8,'gy'=4] {'gx'}, dimensions={1} | all-to-all | bytes 262144 | tf_op jit(solution)/shard_map/all_to_all | solution.py:119
  47.1 3.8 %all-to-all-start.1 = ((s32[2,8,4,512]{3,1,0,2:T(8,128)}), s32[2,8,4,512]{3,1,0,2:T(8,128)S(1)}, u32[]{:S(2)}, u32[]{:S(2)}) async-start(s32[2,8,4,512]{3,1,0,2:T(8,128)} %copy.17), calls=%async_computation.1 | async-start | bytes 262144 | tf_op jit(solution)/shard_map/all_to_all | solution.py:118
  51.5 14.3 %scatter_custom_fusion.1 = f32[16,16384]{0,1:T(8,128)} fusion(s32[4096]{0:T(1024)S(1)} %bitcast.89, f32[4096,16]{1,0:T(8,128)S(1)} %copy.19, f32[]{:T(128)} %constant.79.clone.1), kind=kCustom, calls=%fused_computation.18 | custom fusion | bytes 1048580 | tf_op jit(solution)/shard_map/scatter | solution.py:100
  65.8 6.0 %copy.20 = f32[16,8,4,512]{3,2,0,1:T(4,128)} copy(f32[16,8,4,512]{0,3,2,1:T(8,128)} %bitcast.65) | data formatting | bytes 2097152 | tf_op jit(solution)/shard_map/reshape | solution.py:107
  71.8 5.3 %all-to-all-start.2 = ((f32[16,8,4,512]{3,2,0,1:T(4,128)}), f32[16,8,4,512]{3,2,0,1:T(4,128)S(1)}, u32[]{:S(2)}, u32[]{:S(2)}) async-start(f32[16,8,4,512]{3,2,0,1:T(4,128)} %copy.20), calls=%async_computation.2 | async-start | bytes 2097152 | tf_op jit(solution)/shard_map/all_to_all | solution.py:106
  77.3 25.5 %all-to-all-done.2 = f32[16,8,4,512]{3,2,0,1:T(4,128)S(1)} async-done(((f32[16,8,4,512]{3,2,0,1:T(4,128)}), f32[16,8,4,512]{3,2,0,1:T(4,128)S(1)}, u32[]{:S(2)}, u32[]{:S(2)}) %all-to-all-start.2) | async-done | bytes 1048608 | tf_op jit(solution)/shard_map/all_to_all | solution.py:106
  104.4 3.9 %all-to-all-start.3 = ((f32[16,8,4,512]{3,1,0,2:T(8,128)}), f32[16,8,4,512]{3,1,0,2:T(8,128)S(1)}, u32[]{:S(2)}, u32[]{:S(2)}) async-start(f32[16,8,4,512]{3,1,0,2:T(8,128)} %copy.21), calls=%async_computation.3 | async-start | bytes 2097152 | tf_op jit(solution)/shard_map/all_to_all | solution.py:105
  108.3 75.1 %while.28 = (s32[]{:T(128)}, f32[5,16384]{1,0:T(8,128)S(1)}, f32[5,4096]{1,0:T(8,128)S(1)}, s32[16384]{0:T(1024)S(1)}, s32[]{:T(128)}, /*index=5*/s32[]{:T(128)}, s32[]{:T(128)}, s32[]{:T(128)}) while((s32[]{:T(128)}, f32[5,16384]{1,0:T(8,128)S(1)}, f32[5,4096]{1,0:T(8,128)S(1)}, s32[16384]{0:T(1024)S(1)}, s32[]{:T(128)}, ...), condition=%wide.region_6.7_spmd.clone, body=%wide.region_5.6_spmd.clone.sunk | while | flops 511869440 | bytes 938141 | solution.py:61
  108.3 9.4 %fusion.54 = f32[5,16384]{1,0:T(8,128)S(1)} fusion(s32[16384]{0:T(1024)S(1)} %get-tuple-element.276, s32[512]{0:T(512)S(1)} %iota_add_fusion.5, f32[5,16384]{1,0:T(8,128)S(1)} %get-tuple-element.266, pred[]{:T(512)S(6)} %compare.3, f32[5,4096]{1,0:T(8,128)S(1)} %get-tuple-element.275, s32[]{:T(128)S(6)} %select_n.38), kind=kOutput, calls=%fused_computation.11.clone.1 | convolution fusion | flops 511868928 | bytes 935941 | tf_op jit(solution)/shard_map/while/body/eval_jaxpr/dot_general | solution.py:54
  117.7 9.4 %fusion.54 = f32[5,16384]{1,0:T(8,128)S(1)} fusion(s32[16384]{0:T(1024)S(1)} %get-tuple-element.276, s32[512]{0:T(512)S(1)} %iota_add_fusion.5, f32[5,16384]{1,0:T(8,128)S(1)} %get-tuple-element.266, pred[]{:T(512)S(6)} %compare.3, f32[5,4096]{1,0:T(8,128)S(1)} %get-tuple-element.275, s32[]{:T(128)S(6)} %select_n.38), kind=kOutput, calls=%fused_computation.11.clone.1 | convolution fusion | flops 511868928 | bytes 935941 | tf_op jit(solution)/shard_map/while/body/eval_jaxpr/dot_general | solution.py:54
  127.1 9.4 %fusion.54 = f32[5,16384]{1,0:T(8,128)S(1)} fusion(s32[16384]{0:T(1024)S(1)} %get-tuple-element.276, s32[512]{0:T(512)S(1)} %iota_add_fusion.5, f32[5,16384]{1,0:T(8,128)S(1)} %get-tuple-element.266, pred[]{:T(512)S(6)} %compare.3, f32[5,4096]{1,0:T(8,128)S(1)} %get-tuple-element.275, s32[]{:T(128)S(6)} %select_n.38), kind=kOutput, calls=%fused_computation.11.clone.1 | convolution fusion | flops 511868928 | bytes 935941 | tf_op jit(solution)/shard_map/while/body/eval_jaxpr/dot_general | solution.py:54
  136.5 9.4 %fusion.54 = f32[5,16384]{1,0:T(8,128)S(1)} fusion(s32[16384]{0:T(1024)S(1)} %get-tuple-element.276, s32[512]{0:T(512)S(1)} %iota_add_fusion.5, f32[5,16384]{1,0:T(8,128)S(1)} %get-tuple-element.266, pred[]{:T(512)S(6)} %compare.3, f32[5,4096]{1,0:T(8,128)S(1)} %get-tuple-element.275, s32[]{:T(128)S(6)} %select_n.38), kind=kOutput, calls=%fused_computation.11.clone.1 | convolution fusion | flops 511868928 | bytes 935941 | tf_op jit(solution)/shard_map/while/body/eval_jaxpr/dot_general | solution.py:54
  145.8 9.4 %fusion.54 = f32[5,16384]{1,0:T(8,128)S(1)} fusion(s32[16384]{0:T(1024)S(1)} %get-tuple-element.276, s32[512]{0:T(512)S(1)} %iota_add_fusion.5, f32[5,16384]{1,0:T(8,128)S(1)} %get-tuple-element.266, pred[]{:T(512)S(6)} %compare.3, f32[5,4096]{1,0:T(8,128)S(1)} %get-tuple-element.275, s32[]{:T(128)S(6)} %select_n.38), kind=kOutput, calls=%fused_computation.11.clone.1 | convolution fusion | flops 511868928 | bytes 935941 | tf_op jit(solution)/shard_map/while/body/eval_jaxpr/dot_general | solution.py:54
  155.2 9.4 %fusion.54 = f32[5,16384]{1,0:T(8,128)S(1)} fusion(s32[16384]{0:T(1024)S(1)} %get-tuple-element.276, s32[512]{0:T(512)S(1)} %iota_add_fusion.5, f32[5,16384]{1,0:T(8,128)S(1)} %get-tuple-element.266, pred[]{:T(512)S(6)} %compare.3, f32[5,4096]{1,0:T(8,128)S(1)} %get-tuple-element.275, s32[]{:T(128)S(6)} %select_n.38), kind=kOutput, calls=%fused_computation.11.clone.1 | convolution fusion | flops 511868928 | bytes 935941 | tf_op jit(solution)/shard_map/while/body/eval_jaxpr/dot_general | solution.py:54
  164.6 9.4 %fusion.54 = f32[5,16384]{1,0:T(8,128)S(1)} fusion(s32[16384]{0:T(1024)S(1)} %get-tuple-element.276, s32[512]{0:T(512)S(1)} %iota_add_fusion.5, f32[5,16384]{1,0:T(8,128)S(1)} %get-tuple-element.266, pred[]{:T(512)S(6)} %compare.3, f32[5,4096]{1,0:T(8,128)S(1)} %get-tuple-element.275, s32[]{:T(128)S(6)} %select_n.38), kind=kOutput, calls=%fused_computation.11.clone.1 | convolution fusion | flops 511868928 | bytes 935941 | tf_op jit(solution)/shard_map/while/body/eval_jaxpr/dot_general | solution.py:54
  174.0 9.4 %fusion.54 = f32[5,16384]{1,0:T(8,128)S(1)} fusion(s32[16384]{0:T(1024)S(1)} %get-tuple-element.276, s32[512]{0:T(512)S(1)} %iota_add_fusion.5, f32[5,16384]{1,0:T(8,128)S(1)} %get-tuple-element.266, pred[]{:T(512)S(6)} %compare.3, f32[5,4096]{1,0:T(8,128)S(1)} %get-tuple-element.275, s32[]{:T(128)S(6)} %select_n.38), kind=kOutput, calls=%fused_computation.11.clone.1 | convolution fusion | flops 511868928 | bytes 935941 | tf_op jit(solution)/shard_map/while/body/eval_jaxpr/dot_general | solution.py:54
  193.4 110.3 %while.27 = (s32[]{:T(128)}, f32[5,4096]{1,0:T(8,128)S(1)}, s32[1,16384]{1,0:T(1,128)S(1)}, f32[5,16384]{1,0:T(8,128)S(1)}, s32[]{:T(128)}, /*index=5*/s32[]{:T(128)}, s32[]{:T(128)}, s32[]{:T(128)}) while((s32[]{:T(128)}, f32[5,4096]{1,0:T(8,128)S(1)}, s32[1,16384]{1,0:T(1,128)S(1)}, f32[5,16384]{1,0:T(8,128)S(1)}, s32[]{:T(128)}, ...), condition=%wide.region_10.11_spmd, body=%wide.region_9.10_spmd.sunk | while | flops 511705600 | bytes 610451 | solution.py:80
  193.7 13.7 %fusion.51 = f32[5,4096]{1,0:T(8,128)S(1)} fusion(f32[5,4096]{1,0:T(8,128)S(1)} %get-tuple-element.290, s32[]{:T(128)S(6)} %select_n.37, f32[5,16384]{1,0:T(8,128)S(1)} %get-tuple-element.300, s32[16384]{0:T(1024)S(1)} %bitcast.85, s32[512]{0:T(512)S(1)} %iota_add_fusion.4), kind=kOutput, calls=%fused_computation.7.clone.1 | convolution fusion | flops 511705088 | bytes 608260 | tf_op jit(solution)/shard_map/while/body/eval_jaxpr/dot_general | solution.py:71
  207.4 13.8 %fusion.51 = f32[5,4096]{1,0:T(8,128)S(1)} fusion(f32[5,4096]{1,0:T(8,128)S(1)} %get-tuple-element.290, s32[]{:T(128)S(6)} %select_n.37, f32[5,16384]{1,0:T(8,128)S(1)} %get-tuple-element.300, s32[16384]{0:T(1024)S(1)} %bitcast.85, s32[512]{0:T(512)S(1)} %iota_add_fusion.4), kind=kOutput, calls=%fused_computation.7.clone.1 | convolution fusion | flops 511705088 | bytes 608260 | tf_op jit(solution)/shard_map/while/body/eval_jaxpr/dot_general | solution.py:71
  221.2 13.8 %fusion.51 = f32[5,4096]{1,0:T(8,128)S(1)} fusion(f32[5,4096]{1,0:T(8,128)S(1)} %get-tuple-element.290, s32[]{:T(128)S(6)} %select_n.37, f32[5,16384]{1,0:T(8,128)S(1)} %get-tuple-element.300, s32[16384]{0:T(1024)S(1)} %bitcast.85, s32[512]{0:T(512)S(1)} %iota_add_fusion.4), kind=kOutput, calls=%fused_computation.7.clone.1 | convolution fusion | flops 511705088 | bytes 608260 | tf_op jit(solution)/shard_map/while/body/eval_jaxpr/dot_general | solution.py:71
  234.9 13.8 %fusion.51 = f32[5,4096]{1,0:T(8,128)S(1)} fusion(f32[5,4096]{1,0:T(8,128)S(1)} %get-tuple-element.290, s32[]{:T(128)S(6)} %select_n.37, f32[5,16384]{1,0:T(8,128)S(1)} %get-tuple-element.300, s32[16384]{0:T(1024)S(1)} %bitcast.85, s32[512]{0:T(512)S(1)} %iota_add_fusion.4), kind=kOutput, calls=%fused_computation.7.clone.1 | convolution fusion | flops 511705088 | bytes 608260 | tf_op jit(solution)/shard_map/while/body/eval_jaxpr/dot_general | solution.py:71
  248.7 13.8 %fusion.51 = f32[5,4096]{1,0:T(8,128)S(1)} fusion(f32[5,4096]{1,0:T(8,128)S(1)} %get-tuple-element.290, s32[]{:T(128)S(6)} %select_n.37, f32[5,16384]{1,0:T(8,128)S(1)} %get-tuple-element.300, s32[16384]{0:T(1024)S(1)} %bitcast.85, s32[512]{0:T(512)S(1)} %iota_add_fusion.4), kind=kOutput, calls=%fused_computation.7.clone.1 | convolution fusion | flops 511705088 | bytes 608260 | tf_op jit(solution)/shard_map/while/body/eval_jaxpr/dot_general | solution.py:71
  262.5 13.8 %fusion.51 = f32[5,4096]{1,0:T(8,128)S(1)} fusion(f32[5,4096]{1,0:T(8,128)S(1)} %get-tuple-element.290, s32[]{:T(128)S(6)} %select_n.37, f32[5,16384]{1,0:T(8,128)S(1)} %get-tuple-element.300, s32[16384]{0:T(1024)S(1)} %bitcast.85, s32[512]{0:T(512)S(1)} %iota_add_fusion.4), kind=kOutput, calls=%fused_computation.7.clone.1 | convolution fusion | flops 511705088 | bytes 608260 | tf_op jit(solution)/shard_map/while/body/eval_jaxpr/dot_general | solution.py:71
  276.2 13.8 %fusion.51 = f32[5,4096]{1,0:T(8,128)S(1)} fusion(f32[5,4096]{1,0:T(8,128)S(1)} %get-tuple-element.290, s32[]{:T(128)S(6)} %select_n.37, f32[5,16384]{1,0:T(8,128)S(1)} %get-tuple-element.300, s32[16384]{0:T(1024)S(1)} %bitcast.85, s32[512]{0:T(512)S(1)} %iota_add_fusion.4), kind=kOutput, calls=%fused_computation.7.clone.1 | convolution fusion | flops 511705088 | bytes 608260 | tf_op jit(solution)/shard_map/while/body/eval_jaxpr/dot_general | solution.py:71
  290.0 13.8 %fusion.51 = f32[5,4096]{1,0:T(8,128)S(1)} fusion(f32[5,4096]{1,0:T(8,128)S(1)} %get-tuple-element.290, s32[]{:T(128)S(6)} %select_n.37, f32[5,16384]{1,0:T(8,128)S(1)} %get-tuple-element.300, s32[16384]{0:T(1024)S(1)} %bitcast.85, s32[512]{0:T(512)S(1)} %iota_add_fusion.4), kind=kOutput, calls=%fused_computation.7.clone.1 | convolution fusion | flops 511705088 | bytes 608260 | tf_op jit(solution)/shard_map/while/body/eval_jaxpr/dot_general | solution.py:71
  303.8 2.5 collective-permute-start
  306.3 4.2 %collective-permute-start.1 = (f32[5,1,128]{2,1,0:T(1,128)S(1)}, f32[5,1,128]{2,1,0:T(1,128)S(1)}, u32[]{:S(2)}, u32[]{:S(2)}) collective-permute-start(f32[5,1,128]{2,1,0:T(1,128)S(1)} %get-tuple-element.203), channel_id=1, source_target_pairs={{0,4},{4,8},{8,12},{12,16},{16,20},{20,24},{24,28},{1,5},{5,9},{9,... | collective-permute-start | bytes 7688 | tf_op jit(solution)/shard_map/ppermute | solution.py:16
  312.0 1.9 collective-permute-start.3
  313.9 3.6 %collective-permute-start.2 = (f32[5,34,1]{2,1,0:T(8,128)S(1)}, f32[5,34,1]{2,1,0:T(8,128)S(1)}, u32[]{:S(2)}, u32[]{:S(2)}) collective-permute-start(f32[5,34,1]{2,1,0:T(8,128)S(1)} %get-tuple-element.201), channel_id=1, source_target_pairs={{1,0},{2,1},{3,2},{5,4},{6,5},{7,6},{9,8},{10,9},{11,10},{13,12},{... | collective-permute-start | bytes 2048 | tf_op jit(solution)/shard_map/ppermute | solution.py:17
  (82 shorter events, 23.3 us)
Async XLA Ops:
  0.6 183.5 %copy-start = (f32[8,16]{1,0:T(8,128)S(1)}, f32[8,16]{1,0:T(8,128)}, u32[]{:S(2)}) copy-start(f32[8,16]{1,0:T(8,128)} %param.15) | copy-start | bytes 1540
  15.1 35.8 %copy-start.2 = (f32[16,4096]{1,0:T(8,128)S(1)}, f32[16,4096]{1,0:T(8,128)}, u32[]{:S(2)}) copy-start(f32[16,4096]{1,0:T(8,128)} %param.11) | copy-start | bytes 786436
  47.1 24.8 %all-to-all-start.1 = ((s32[2,8,4,512]{3,1,0,2:T(8,128)}), s32[2,8,4,512]{3,1,0,2:T(8,128)S(1)}, u32[]{:S(2)}, u32[]{:S(2)}) async-start(s32[2,8,4,512]{3,1,0,2:T(8,128)} %copy.17), calls=%async_computation.1 | async-start | bytes 262144 | tf_op jit(solution)/shard_map/all_to_all | solution.py:118
  51.5 25.6 %copy-start.3 = (f32[4,32,128]{2,1,0:T(8,128)S(1)}, f32[4,32,128]{2,1,0:T(8,128)}, u32[]{:S(2)}) copy-start(f32[4,32,128]{2,1,0:T(8,128)} %param.17) | copy-start | bytes 196612
  51.5 25.7 %copy-start.4 = (f32[32,128]{1,0:T(8,128)S(1)}, f32[32,128]{1,0:T(8,128)}, u32[]{:S(2)}) copy-start(f32[32,128]{1,0:T(8,128)} %param.16) | copy-start | bytes 49156
  71.8 31.0 %all-to-all-start.2 = ((f32[16,8,4,512]{3,2,0,1:T(4,128)}), f32[16,8,4,512]{3,2,0,1:T(4,128)S(1)}, u32[]{:S(2)}, u32[]{:S(2)}) async-start(f32[16,8,4,512]{3,2,0,1:T(4,128)} %copy.20), calls=%async_computation.2 | async-start | bytes 2097152 | tf_op jit(solution)/shard_map/all_to_all | solution.py:106
  104.4 80.4 %all-to-all-start.3 = ((f32[16,8,4,512]{3,1,0,2:T(8,128)}), f32[16,8,4,512]{3,1,0,2:T(8,128)S(1)}, u32[]{:S(2)}, u32[]{:S(2)}) async-start(f32[16,8,4,512]{3,1,0,2:T(8,128)} %copy.21), calls=%async_computation.3 | async-start | bytes 2097152 | tf_op jit(solution)/shard_map/all_to_all | solution.py:105
  183.4 0.8 copy-start.1
  193.4 126.5 %copy-start.5 = (f32[32,128]{1,0:T(8,128)S(1)}, f32[32,128]{1,0:T(8,128)}, u32[]{:S(2)}) copy-start(f32[32,128]{1,0:T(8,128)} %param.16) | copy-start | bytes 49156
  303.8 6.8 %collective-permute-start = (f32[5,1,128]{2,1,0:T(1,128)S(1)}, f32[5,1,128]{2,1,0:T(1,128)S(1)}, u32[]{:S(2)}, u32[]{:S(2)}) collective-permute-start(f32[5,1,128]{2,1,0:T(1,128)S(1)} %get-tuple-element.204), channel_id=1, source_target_pairs={{4,0},{8,4},{12,8},{16,12},{20,16},{24,20},{28,24},{5,1},{9,5},{13... | collective-permute-start | bytes 7688 | tf_op jit(solution)/shard_map/ppermute | solution.py:17
  306.3 5.5 %collective-permute-start.1 = (f32[5,1,128]{2,1,0:T(1,128)S(1)}, f32[5,1,128]{2,1,0:T(1,128)S(1)}, u32[]{:S(2)}, u32[]{:S(2)}) collective-permute-start(f32[5,1,128]{2,1,0:T(1,128)S(1)} %get-tuple-element.203), channel_id=1, source_target_pairs={{0,4},{4,8},{8,12},{12,16},{16,20},{20,24},{24,28},{1,5},{5,9},{9,... | collective-permute-start | bytes 7688 | tf_op jit(solution)/shard_map/ppermute | solution.py:16
  312.0 6.0 %collective-permute-start.3 = (f32[5,34,1]{2,1,0:T(8,128)S(1)}, f32[5,34,1]{2,1,0:T(8,128)S(1)}, u32[]{:S(2)}, u32[]{:S(2)}) collective-permute-start(f32[5,34,1]{2,1,0:T(8,128)S(1)} %get-tuple-element.202), channel_id=1, source_target_pairs={{0,1},{1,2},{2,3},{4,5},{5,6},{6,7},{8,9},{9,10},{10,11},{12,13},{... | collective-permute-start | bytes 2048 | tf_op jit(solution)/shard_map/ppermute | solution.py:16
  313.9 5.9 %collective-permute-start.2 = (f32[5,34,1]{2,1,0:T(8,128)S(1)}, f32[5,34,1]{2,1,0:T(8,128)S(1)}, u32[]{:S(2)}, u32[]{:S(2)}) collective-permute-start(f32[5,34,1]{2,1,0:T(8,128)S(1)} %get-tuple-element.201), channel_id=1, source_target_pairs={{1,0},{2,1},{3,2},{5,4},{6,5},{7,6},{9,8},{10,9},{11,10},{13,12},{... | collective-permute-start | bytes 2048 | tf_op jit(solution)/shard_map/ppermute | solution.py:17
where the time goes:
time: 326 us; the launch traced here: 321 us
  matrix products  186 us (57%)
  local copies, waits for them, and re-layouts  48.9 us (15%)
  waiting for transfers between devices  29 us (9%)
  starting transfers between devices  25.2 us (8%)
  other arithmetic  19.4 us (6%)
  blocking collectives  11.7 us (4%)
    dot_general x8, matrix products, deposit_advance(): lax.dot_general(source, cell_hot(cells, first, width), (((1,), (1,)), (()...  110 us
    dot_general x8, matrix products, look_advance(): jnp.dot(block, cell_hot(cells, first, width), precision=lax.Precision.HIG...  75 us
    all_to_all x1, waiting for transfers between devices, per_device(): lax.all_to_all(float_buf.reshape(-1, width_x, width_y, capacity), 'gx', s...  25.5 us
    scatter x1, local copies, waits for them, and re-layouts, per_device(): jnp.full((2, slots), -1, jnp.int32).at[:, slot]  14.3 us
    scatter x1, local copies, waits for them, and re-layouts, per_device(): jnp.zeros((parcel_props.shape[0], slots), jnp.float32).at[:, slot]  14.3 us
    all_to_all x1, blocking collectives, per_device(): lax.all_to_all(int_buf.reshape(2, width_x, width_y, capacity), 'gx', spli...  11.7 us
    another operation x3, other arithmetic  9.62 us
  transfers between devices with their start and end apart: 7, of which 4 were waited for; matrix products, arithmetic and copies ran while one was open for 30% of the time, Pallas kernels for 0%

commit v1 on v0

v1 whole, which is shorter than its diff:
```python
import math

import jax
import jax.numpy as jnp
from jax import lax
from jax.experimental import pallas as pl
from jax.experimental.pallas import tpu as pltpu
from jax.sharding import PartitionSpec as P

F32, BF16, I32 = jnp.float32, jnp.bfloat16, jnp.int32
NT = (((1,), (1,)), ((), ()))
LANES = 256
VALUES = 8


def shift_of(n):
    assert n & (n - 1) == 0
    return n.bit_length() - 1


def split2(x):
    top = x.astype(BF16)
    return top, (x - top.astype(F32)).astype(BF16)


def hot(rows, row):
    kinds = lax.broadcasted_iota(I32, (rows, row.shape[1]), 0)
    return (kinds == row).astype(F32).astype(BF16)


def bucket_kernel(props_ref, cls_ref, own_ref, cell_ref, tab_ref, out_ref, a_ref, *, devices, cap, lw):
    n = props_ref.shape[1]
    slots = devices * cap
    his = slots // lw
    tri = (
        lax.broadcasted_iota(I32, (LANES, LANES), 0) < lax.broadcasted_iota(I32, (LANES, LANES), 1)
    ).astype(F32).astype(BF16)
    carry = (lax.broadcasted_iota(I32, (devices, 1), 0) * cap).astype(F32)
    slot = []
    for k in range(n // LANES):
        own = own_ref[:, k * LANES : (k + 1) * LANES]
        member = (lax.broadcasted_iota(I32, (devices, LANES), 0) == own).astype(F32)
        before = jnp.dot(member.astype(BF16), tri, preferred_element_type=F32)
        slot.append(jnp.sum(member * (before + carry), axis=0, keepdims=True))
        carry = carry + jnp.sum(member, axis=1, keepdims=True)
    slot = jnp.concatenate(slot, axis=1).astype(I32)
    hi = lax.shift_right_logical(slot, shift_of(lw))
    lo = slot & (lw - 1)
    table = tab_ref[...]
    col = lax.broadcasted_iota(I32, table.shape, 1)
    table = jnp.where(col > 4, table, jnp.where(col == 4, 1.0, 0.0))
    mixed = jnp.dot(
        table, props_ref[...], precision=lax.Precision.HIGHEST, preferred_element_type=F32
    )
    kinds = lax.broadcasted_iota(I32, mixed.shape, 0)
    total = jnp.sum(jnp.where(kinds == cls_ref[...], mixed, 0.0), axis=0, keepdims=True)
    vals = props_ref[0:VALUES, :]
    row = lax.broadcasted_iota(I32, vals.shape, 0)
    vals = jnp.where(row == 0, jnp.exp(0.5 * vals), vals)
    vals = jnp.where(row == 5, total, vals)
    vals = jnp.where(row == 6, cls_ref[...].astype(F32), vals)
    vals = jnp.where(row == 7, cell_ref[...].astype(F32), vals)
    top, low = split2(vals)
    pair = jnp.concatenate([top, low], axis=0)
    low_hot = hot(lw, lo)
    hi_b = jnp.broadcast_to(hi.astype(F32), (2 * VALUES, n)).astype(BF16)
    zero = jnp.zeros_like(pair)
    block = min(his, 32)
    for b in range(his // block):
        for h in range(block):
            a_ref[h * 2 * VALUES : (h + 1) * 2 * VALUES, :] = jnp.where(
                hi_b == jnp.asarray(b * block + h, BF16), pair, zero
            )
        placed = lax.dot_general(a_ref[...], low_hot, NT, preferred_element_type=F32)
        placed = placed.reshape(block, 2, VALUES, lw)
        out_ref[b * block : (b + 1) * block] = placed[:, 0] + placed[:, 1]


def owner_kernel(
    x_ref, tab_ref, rho_ref, rest_ref, dep_ref, g_ref, y_ref, a_ref, acc_ref, s_ref
):
    slab_x, slab_y = rho_ref.shape
    fold = LANES // slab_y
    xs = slab_x // fold
    classes = tab_ref.shape[0]
    for f in range(fold):
        rho = rho_ref[pl.ds(f, xs, stride=fold), :]
        for c in range(4):
            ratio = rest_ref[c, pl.ds(f, xs, stride=fold), :] / rho
            top, low = split2(ratio)
            g_ref[c * xs : (c + 1) * xs, f * slab_y : (f + 1) * slab_y] = top
            g_ref[(4 + c) * xs : (5 + c) * xs, f * slab_y : (f + 1) * slab_y] = low
    acc_ref[...] = jnp.zeros_like(acc_ref)
    half = LANES // 2
    s_ref[0] = x_ref[:, :half]
    s_ref[1] = x_ref[:, half:]
    rows = 8
    groups = x_ref.shape[0] // (rows * VALUES)
    y_shift = shift_of(LANES)

    def group(g, _):
        base = g * (rows * VALUES)
        mass, q1, q2, q3, q4, total, cls, cell = [
            jnp.concatenate(
                [s_ref[i, pl.ds(base + v, rows, stride=VALUES), :] for i in range(2)], axis=1
            )
            for v in range(VALUES)
        ]
        cell = cell.astype(I32)
        cell_x = lax.shift_right_logical(cell, y_shift)
        cell_y = cell & (LANES - 1)
        gas = [[] for _ in range(4)]
        masks = []
        for r in range(rows):
            y_hot = hot(LANES, cell_y[r : r + 1])
            y_ref[:, r * LANES : (r + 1) * LANES] = y_hot
            found = jnp.dot(g_ref[...], y_hot, preferred_element_type=F32)
            mask = lax.broadcasted_iota(I32, (xs, LANES), 0) == cell_x[r : r + 1]
            masks.append(mask)
            for c in range(4):
                both = found[c * xs : (c + 1) * xs] + found[(4 + c) * xs : (5 + c) * xs]
                gas[c].append(jnp.sum(jnp.where(mask, both, 0.0), axis=0, keepdims=True))
        v1, v2, v3, theta = [jnp.concatenate(part, axis=0) for part in gas]
        coef = []
        for j in range(5):
            picked = jnp.full(cls.shape, tab_ref[0, j], F32)
            for k in range(1, classes):
                picked = jnp.where(cls == float(k), tab_ref[k, j], picked)
            coef.append(picked)
        w1, w2, w3 = q1 - v1, q2 - v2, q3 - v3
        heat = q4 - theta
        soft = jnp.maximum(heat, 0.0) + jnp.log1p(jnp.exp(-jnp.abs(heat)))
        evapor = mass * (1.0 - jnp.exp(-(coef[0] * soft)))
        dragged = 1.0 - jnp.exp(-coef[1] * jnp.sqrt(1.0 + (w1 * w1 + w2 * w2 + w3 * w3)))
        drag = mass * dragged
        source = [
            evapor,
            evapor * coef[2] * q1 + drag * w1,
            evapor * coef[3] * q2 + drag * w2,
            evapor * coef[4] * q3 + drag * w3,
            evapor * total,
        ]
        for c in range(5):
            for r in range(rows):
                line = jnp.where(masks[r], source[c][r : r + 1], 0.0)
                top, low = split2(line)
                a_ref[c * xs : (c + 1) * xs, r * LANES : (r + 1) * LANES] = top
                a_ref[(5 + c) * xs : (6 + c) * xs, r * LANES : (r + 1) * LANES] = low
        acc_ref[...] += lax.dot_general(a_ref[...], y_ref[...], NT, preferred_element_type=F32)
        return 0

    lax.fori_loop(0, groups, group, 0)
    for c in range(5):
        both = acc_ref[c * xs : (c + 1) * xs, :] + acc_ref[(5 + c) * xs : (6 + c) * xs, :]
        for f in range(fold):
            dep_ref[c, pl.ds(f, xs, stride=fold), :] = both[:, f * slab_y : (f + 1) * slab_y]


def shifted(edge, axis, step):
    devices = lax.axis_size(axis)
    pairs = [(i, i + step) for i in range(devices) if 0 <= i + step < devices]
    return lax.ppermute(edge, axis, pairs)


def per_device(
    parcel_props, size_class, dest_owner, dest_local, class_table, gas_density, gas_rest
):
    devices = lax.axis_size("gx") * lax.axis_size("gy")
    props, parcels = parcel_props.shape
    slab_x, slab_y = gas_density.shape
    cap = max(2, 4 * parcels // devices)
    slots = devices * cap
    lw = math.gcd(cap, LANES)
    his = slots // lw
    vmem = pl.BlockSpec(memory_space=pltpu.VMEM)
    smem = pl.BlockSpec(memory_space=pltpu.SMEM)
    sent = pl.pallas_call(
        lambda *refs: bucket_kernel(*refs, devices=devices, cap=cap, lw=lw),
        out_shape=jax.ShapeDtypeStruct((his, VALUES, lw), F32),
        in_specs=[vmem] * 5,
        out_specs=vmem,
        scratch_shapes=[pltpu.VMEM((min(his, 32) * 2 * VALUES, parcels), BF16)],
        name="bucket",
    )(
        parcel_props,
        size_class.reshape(1, parcels),
        dest_owner.reshape(1, parcels),
        dest_local.reshape(1, parcels),
        class_table,
    )
    got = lax.all_to_all(sent, ("gx", "gy"), split_axis=0, concat_axis=0, tiled=True)
    if lw != LANES:
        got = got.reshape(slots // LANES, LANES // lw, VALUES, lw).transpose(0, 2, 1, 3)
    xs = slab_x * slab_y // LANES
    deposit = pl.pallas_call(
        owner_kernel,
        out_shape=jax.ShapeDtypeStruct((5, slab_x, slab_y), F32),
        in_specs=[vmem, smem, vmem, vmem],
        out_specs=vmem,
        scratch_shapes=[
            pltpu.VMEM((8 * xs, LANES), BF16),
            pltpu.VMEM((LANES, 8 * LANES), BF16),
            pltpu.VMEM((10 * xs, 8 * LANES), BF16),
            pltpu.VMEM((10 * xs, LANES), F32),
            pltpu.VMEM((2, slots // LANES * VALUES, LANES // 2), F32),
        ],
        name="owner",
    )(got.reshape(slots // LANES * VALUES, LANES), class_table, gas_density, gas_rest)
    above = shifted(deposit[:, -1:, :], "gx", 1)
    below = shifted(deposit[:, :1, :], "gx", -1)
    left = shifted(deposit[:, :, -1:], "gy", 1)
    right = shifted(deposit[:, :, :1], "gy", -1)
    tall = jnp.concatenate([above, deposit, below], axis=1)
    wide = jnp.concatenate([left, deposit, right], axis=2)
    beside = tall[:, 2:] + tall[:, :-2] + wide[:, :, 2:] + wide[:, :, :-2]
    smooth = 0.4 * deposit + 0.15 * beside
    return (gas_density + smooth[0], gas_rest + smooth[1:])


def solution(mesh):
    return jax.shard_map(
        per_device,
        mesh=mesh,
        in_specs=(
            P(None, ("gx", "gy")),
            P(("gx", "gy")),
            P(("gx", "gy"), None),
            P(("gx", "gy")),
            P(),
            P("gx", "gy"),
            P(None, "gx", "gy"),
        ),
        out_specs=(P("gx", "gy"), P(None, "gx", "gy")),
        check_vma=False,
    )
```

time: 326 us -> 53.6 us (0.16); the launches traced: 321 us -> 53.1 us
  matrix products: 186 us -> 0 us
  local copies, waits for them, and re-layouts: 48.9 us -> 1.88 us
  waiting for transfers between devices: 29 us -> 3.34 us
  other arithmetic: 19.4 us -> 1.38 us
  starting transfers between devices: 25.2 us -> 11.2 us
  Pallas kernels: 0 us -> 13.7 us
  blocking collectives: 11.7 us -> 20.9 us
    dot_general x17 -> x0, matrix products: 186 us -> none  [the longest x8 110 us: deposit_advance(): lax.dot_general(source, cell_hot(cells, first, width), (((1,), (1,)), (()...]
    scatter x2 -> x0, local copies, waits for them, and re-layouts: 28.6 us -> none  [the longest x1 14.3 us: per_device(): jnp.full((2, slots), -1, jnp.int32).at[:, slot]]
    all_to_all x3 -> x0, waiting for transfers between devices: 25.5 us -> none  [the longest x1 25.5 us: per_device(): lax.all_to_all(float_buf.reshape(-1, width_x, width_y, capacity), 'gx', s...]
    pallas_call x0 -> x2, Pallas kernels: none -> 13.7 us  [the longest x1 8.87 us: per_device(): pl.pallas_call(owner_kernel, out_shape=jax.ShapeDtypeStruct((5, slab_x, s...]
    all_to_all x3 -> x0, starting transfers between devices: 12.9 us -> none  [the longest x1 5.27 us: per_device(): lax.all_to_all(float_buf.reshape(-1, width_x, width_y, capacity), 'gx', s...]
    reshape x2 -> x0, local copies, waits for them, and re-layouts: 11.2 us -> none  [the longest x1 6.02 us: per_device(): float_buf.reshape(-1, width_x, width_y, capacity)]
    another operation x4 -> x0, other arithmetic: 10.4 us -> none
    all_to_all x1, blocking collectives: 11.7 us -> 20.9 us  [per_device(): lax.all_to_all(sent, ('gx', 'gy'), split_axis=0, concat_axis=0, tiled=True)]
  transfers between devices with their start and end apart: 7 -> 4, of which waited for: 4 -> 1; matrix products, arithmetic and copies ran while one was open for 30% -> 2% of each run, Pallas kernels for 0% -> 0%
where the time goes in v1:
time: 53.6 us; the launch traced here: 53.1 us
  blocking collectives  20.9 us (39%)
  Pallas kernels  13.7 us (26%)
  starting transfers between devices  11.2 us (21%)
  waiting for transfers between devices  3.34 us (6%)
  local copies, waits for them, and re-layouts  1.88 us (4%)
  other arithmetic  1.38 us (3%)
  between operations  0.72 us (1%)
    all_to_all x1, blocking collectives, per_device(): lax.all_to_all(sent, ('gx', 'gy'), split_axis=0, concat_axis=0, tiled=True)  20.9 us
    ppermute x4, starting transfers between devices, shifted(): return lax.ppermute(edge, axis, pairs)  11.2 us
    pallas_call x1, Pallas kernels, per_device(): pl.pallas_call(owner_kernel, out_shape=jax.ShapeDtypeStruct((5, slab_x, s...  8.87 us
    pallas_call x1, Pallas kernels, per_device(): pl.pallas_call(lambda *refs: bucket_kernel(*refs, devices=devices, cap=ca...  4.81 us
    ppermute x4, waiting for transfers between devices, shifted(): return lax.ppermute(edge, axis, pairs)  3.34 us
    add x2, other arithmetic, per_device(): return (gas_density + smooth[0], gas_rest + smooth[1:])  1.25 us
  transfers between devices with their start and end apart: 4, of which 1 were waited for; matrix products, arithmetic and copies ran while one was open for 2% of the time, Pallas kernels for 0%

profile of v1, /device:TPU:6, one launch (start us, length us, event | category | flops | bytes accessed | tf_op | source)
XLA Modules:
  0.0 53.1 jit_solution(780784699103839984)
XLA Ops:
  0.6 4.8 %bucket.1 = f32[64,8,256]{2,1,0:T(8,128)} custom-call(f32[16,4096]{1,0:T(8,128)} %refs_0_.1, s32[1,4096]{1,0:T(1,128)} %bitcast.9, s32[1,4096]{1,0:T(1,128)} %bitcast.10, s32[1,4096]{1,0:T(1,128)} %bitcast.11, f32[8,16]{1,0:T(8,128)} %tab_ref.1), custom_call_target="tpu_custom_call" | custom-call | tf_op jit(solution)/shard_map/bucket/pallas_call | solution.py:177
  5.4 20.9 %all_to_all.5 = f32[64,8,256]{2,1,0:T(8,128)} all-to-all(f32[64,8,256]{2,1,0:T(8,128)} %bucket.1), channel_id=1, replica_groups=mesh['gx'=8,'gy'=4] {'gx','gy'}, dimensions={0} | all-to-all | bytes 1048576 | tf_op jit(solution)/shard_map/all_to_all | solution.py:191
  26.3 8.9 %owner.1 = f32[5,32,128]{2,1,0:T(8,128)} custom-call(f32[512,256]{1,0:T(8,128)} %bitcast.8, f32[8,16]{1,0:T(8,128)} %tab_ref.1, f32[32,128]{1,0:T(8,128)} %rho_ref.1, f32[4,32,128]{2,1,0:T(8,128)} %rest_ref.1), custom_call_target="tpu_custom_call" | custom-call | tf_op jit(solution)/shard_map/owner/pallas_call | solution.py:195
  35.2 0.7 %fusion.6 = (f32[5,1,128]{2,1,0:T(1,128)S(1)}, f32[5,1,128]{2,1,0:T(1,128)S(1)}) fusion(f32[5,32,128]{2,1,0:T(8,128)} %owner.1), kind=kLoop, calls=%fused_computation.12 | loop fusion | bytes 10240 | tf_op jit(solution)/shard_map/slice | solution.py:210
  36.0 2.4 %collective-permute-start = (f32[5,1,128]{2,1,0:T(1,128)S(1)}, f32[5,1,128]{2,1,0:T(1,128)S(1)}, u32[]{:S(2)}, u32[]{:S(2)}) collective-permute-start(f32[5,1,128]{2,1,0:T(1,128)S(1)} %get-tuple-element.2), channel_id=1, source_target_pairs={{4,0},{8,4},{12,8},{16,12},{20,16},{24,20},{28,24},{5,1},{9,5},{13... | collective-permute-start | bytes 7688 | tf_op jit(solution)/shard_map/ppermute | solution.py:162
  38.4 0.0 copy-start
  38.4 4.4 %collective-permute-start.1 = (f32[5,1,128]{2,1,0:T(1,128)S(1)}, f32[5,1,128]{2,1,0:T(1,128)S(1)}, u32[]{:S(2)}, u32[]{:S(2)}) collective-permute-start(f32[5,1,128]{2,1,0:T(1,128)S(1)} %get-tuple-element.3), channel_id=1, source_target_pairs={{0,4},{4,8},{8,12},{12,16},{16,20},{20,24},{24,28},{1,5},{5,9},{9,... | collective-permute-start | bytes 7688 | tf_op jit(solution)/shard_map/ppermute | solution.py:162
  42.8 1.0 %fusion.7 = (f32[5,32,1]{2,1,0:T(8,128)S(1)}, f32[5,32,1]{2,1,0:T(8,128)S(1)}) fusion(f32[5,32,128]{2,1,0:T(8,128)} %owner.1), kind=kLoop, calls=%fused_computation.13 | loop fusion | bytes 2560 | tf_op jit(solution)/shard_map/slice | solution.py:212
  43.9 1.9 %collective-permute-start.2 = (f32[5,32,1]{2,1,0:T(8,128)S(1)}, f32[5,32,1]{2,1,0:T(8,128)S(1)}, u32[]{:S(2)}, u32[]{:S(2)}) collective-permute-start(f32[5,32,1]{2,1,0:T(8,128)S(1)} %get-tuple-element.4), channel_id=1, source_target_pairs={{1,0},{2,1},{3,2},{5,4},{6,5},{7,6},{9,8},{10,9},{11,10},{13,12},{... | collective-permute-start | bytes 1928 | tf_op jit(solution)/shard_map/ppermute | solution.py:162
  45.8 0.0 copy-start.2
  45.8 2.4 %collective-permute-start.3 = (f32[5,32,1]{2,1,0:T(8,128)S(1)}, f32[5,32,1]{2,1,0:T(8,128)S(1)}, u32[]{:S(2)}, u32[]{:S(2)}) collective-permute-start(f32[5,32,1]{2,1,0:T(8,128)S(1)} %get-tuple-element.5), channel_id=1, source_target_pairs={{0,1},{1,2},{2,3},{4,5},{5,6},{6,7},{8,9},{9,10},{10,11},{12,13},{... | collective-permute-start | bytes 1928 | tf_op jit(solution)/shard_map/ppermute | solution.py:162
  48.2 0.0 collective-permute-done.2
  48.3 3.3 %collective-permute-done.3 = f32[5,32,1]{2,1,0:T(8,128)S(1)} collective-permute-done((f32[5,32,1]{2,1,0:T(8,128)S(1)}, f32[5,32,1]{2,1,0:T(8,128)S(1)}, u32[]{:S(2)}, u32[]{:S(2)}) %collective-permute-start.3) | collective-permute-done | bytes 672 | tf_op jit(solution)/shard_map/ppermute | solution.py:162
  51.6 0.0 collective-permute-done
  51.6 0.0 collective-permute-done.1
  51.6 0.0 copy-done
  51.6 0.0 copy-start.1
  51.6 0.1 fusion.2
  51.8 0.0 copy-done.2
  51.8 0.6 %fusion.5 = f32[32,128]{1,0:T(8,128)} fusion(f32[32,128]{1,0:T(8,128)S(1)} %copy-done.2, f32[5,32,128]{2,1,0:T(8,128)S(1)} %fusion.2), kind=kLoop, calls=%fused_computation.11 | loop fusion | flops 4096 | bytes 49152 | tf_op jit(solution)/shard_map/add | solution.py:217
  52.4 0.1 copy-done.1
  52.4 0.6 %slice_add_fusion = f32[4,32,128]{2,1,0:T(8,128)} fusion(f32[4,32,128]{2,1,0:T(8,128)S(1)} %copy-done.1, f32[5,32,128]{2,1,0:T(8,128)S(1)} %fusion.2), kind=kLoop, calls=%fused_computation.9 | loop fusion | flops 16384 | bytes 196608 | tf_op jit(solution)/shard_map/add | solution.py:217
Async XLA Ops:
  36.0 15.6 %collective-permute-start = (f32[5,1,128]{2,1,0:T(1,128)S(1)}, f32[5,1,128]{2,1,0:T(1,128)S(1)}, u32[]{:S(2)}, u32[]{:S(2)}) collective-permute-start(f32[5,1,128]{2,1,0:T(1,128)S(1)} %get-tuple-element.2), channel_id=1, source_target_pairs={{4,0},{8,4},{12,8},{16,12},{20,16},{24,20},{28,24},{5,1},{9,5},{13... | collective-permute-start | bytes 7688 | tf_op jit(solution)/shard_map/ppermute | solution.py:162
  38.4 13.2 %copy-start = (f32[5,32,128]{2,1,0:T(8,128)S(1)}, f32[5,32,128]{2,1,0:T(8,128)}, u32[]{:S(2)}) copy-start(f32[5,32,128]{2,1,0:T(8,128)} %owner.1) | copy-start | bytes 245764
  38.4 13.2 %collective-permute-start.1 = (f32[5,1,128]{2,1,0:T(1,128)S(1)}, f32[5,1,128]{2,1,0:T(1,128)S(1)}, u32[]{:S(2)}, u32[]{:S(2)}) collective-permute-start(f32[5,1,128]{2,1,0:T(1,128)S(1)} %get-tuple-element.3), channel_id=1, source_target_pairs={{0,4},{4,8},{8,12},{12,16},{16,20},{20,24},{24,28},{1,5},{5,9},{9,... | collective-permute-start | bytes 7688 | tf_op jit(solution)/shard_map/ppermute | solution.py:162
  43.9 4.4 %collective-permute-start.2 = (f32[5,32,1]{2,1,0:T(8,128)S(1)}, f32[5,32,1]{2,1,0:T(8,128)S(1)}, u32[]{:S(2)}, u32[]{:S(2)}) collective-permute-start(f32[5,32,1]{2,1,0:T(8,128)S(1)} %get-tuple-element.4), channel_id=1, source_target_pairs={{1,0},{2,1},{3,2},{5,4},{6,5},{7,6},{9,8},{10,9},{11,10},{13,12},{... | collective-permute-start | bytes 1928 | tf_op jit(solution)/shard_map/ppermute | solution.py:162
  45.8 5.9 %copy-start.2 = (f32[32,128]{1,0:T(8,128)S(1)}, f32[32,128]{1,0:T(8,128)}, u32[]{:S(2)}) copy-start(f32[32,128]{1,0:T(8,128)} %rho_ref.1) | copy-start | bytes 49156
  45.8 5.8 %collective-permute-start.3 = (f32[5,32,1]{2,1,0:T(8,128)S(1)}, f32[5,32,1]{2,1,0:T(8,128)S(1)}, u32[]{:S(2)}, u32[]{:S(2)}) collective-permute-start(f32[5,32,1]{2,1,0:T(8,128)S(1)} %get-tuple-element.5), channel_id=1, source_target_pairs={{0,1},{1,2},{2,3},{4,5},{5,6},{6,7},{8,9},{9,10},{10,11},{12,13},{... | collective-permute-start | bytes 1928 | tf_op jit(solution)/shard_map/ppermute | solution.py:162
  51.6 0.8 %copy-start.1 = (f32[4,32,128]{2,1,0:T(8,128)S(1)}, f32[4,32,128]{2,1,0:T(8,128)}, u32[]{:S(2)}) copy-start(f32[4,32,128]{2,1,0:T(8,128)} %rest_ref.1) | copy-start | bytes 196612

commit v2 on v1

--- a/solution.py
+++ b/solution.py
@@ -156,10 +156,16 @@
             dep_ref[c, pl.ds(f, xs, stride=fold), :] = both[:, f * slab_y : (f + 1) * slab_y]
 
 
-def shifted(edge, axis, step):
+def exchanged(first, last, axis):
     devices = lax.axis_size(axis)
-    pairs = [(i, i + step) for i in range(devices) if 0 <= i + step < devices]
-    return lax.ppermute(edge, axis, pairs)
+    even = lax.axis_index(axis) % 2 == 0
+    got = []
+    for start in (0, 1):
+        pairs = [(i, i + 1) for i in range(start, devices - 1, 2)]
+        pairs = pairs + [(j, i) for i, j in pairs]
+        lower = even if start == 0 else jnp.logical_not(even)
+        got.append(lax.ppermute(jnp.where(lower, last, first), axis, pairs))
+    return jnp.where(even, got[1], got[0]), jnp.where(even, got[0], got[1])
 
 
 def per_device(
@@ -206,10 +212,8 @@
         ],
         name="owner",
     )(got.reshape(slots // LANES * VALUES, LANES), class_table, gas_density, gas_rest)
-    above = shifted(deposit[:, -1:, :], "gx", 1)
-    below = shifted(deposit[:, :1, :], "gx", -1)
-    left = shifted(deposit[:, :, -1:], "gy", 1)
-    right = shifted(deposit[:, :, :1], "gy", -1)
+    left, right = exchanged(deposit[:, :, :1], deposit[:, :, -1:], "gy")
+    above, below = exchanged(deposit[:, :1, :], deposit[:, -1:, :], "gx")
     tall = jnp.concatenate([above, deposit, below], axis=1)
     wide = jnp.concatenate([left, deposit, right], axis=2)
     beside = tall[:, 2:] + tall[:, :-2] + wide[:, :, 2:] + wide[:, :, :-2]

time: 53.6 us -> 49.6 us (0.925)
  blocking collectives: 20.9 us -> 0 us
  waiting for transfers between devices: 3.34 us -> 17.7 us
  starting transfers between devices: 11.2 us -> 13.2 us
  other arithmetic: 1.38 us -> 2.53 us
    all_to_all x1 -> x0, blocking collectives: 20.9 us -> none  [per_device(): lax.all_to_all(sent, ('gx', 'gy'), split_axis=0, concat_axis=0, tiled=True)]
    all_to_all x0 -> x1, waiting for transfers between devices: none -> 14.7 us  [per_device(): lax.all_to_all(sent, ('gx', 'gy'), split_axis=0, concat_axis=0, tiled=True)]
    all_to_all x0 -> x1, starting transfers between devices: none -> 6.08 us  [per_device(): lax.all_to_all(sent, ('gx', 'gy'), split_axis=0, concat_axis=0, tiled=True)]
    ppermute x4, starting transfers between devices: 11.2 us -> 7.15 us  [exchanged(): got.append(lax.ppermute(jnp.where(lower, last, first), axis, pairs))]
    slice x2 -> x0, local copies, waits for them, and re-layouts: 1.79 us -> none  [the longest x1 1.05 us: per_device(): right = shifted(deposit[:, :, :1], 'gy', -1)]
    unnamed x6 -> x8, local copies, waits for them, and re-layouts: 0.09 us -> 1.37 us
    select_n x0 -> x4, other arithmetic: none -> 1.15 us  [the longest x2 1.13 us: exchanged(): got.append(lax.ppermute(jnp.where(lower, last, first), axis, pairs))]
  transfers between devices with their start and end apart: 4 -> 5, of which waited for: 1 -> 2; matrix products, arithmetic and copies ran while one was open for 2% -> 0% of each run, Pallas kernels for 0% -> 0%
where the time goes in v2:
time: 49.6 us; the launch traced here: 49.3 us
  waiting for transfers between devices  17.7 us (36%)
  Pallas kernels  13.7 us (28%)
  starting transfers between devices  13.2 us (27%)
  other arithmetic  2.53 us (5%)
  local copies, waits for them, and re-layouts  1.37 us (3%)
  between operations  0.76 us (2%)
    all_to_all x1, waiting for transfers between devices, per_device(): lax.all_to_all(sent, ('gx', 'gy'), split_axis=0, concat_axis=0, tiled=True)  14.7 us
    pallas_call x1, Pallas kernels, per_device(): pl.pallas_call(owner_kernel, out_shape=jax.ShapeDtypeStruct((5, slab_x, s...  8.86 us
    ppermute x4, starting transfers between devices, exchanged(): got.append(lax.ppermute(jnp.where(lower, last, first), axis, pairs))  7.15 us
    all_to_all x1, starting transfers between devices, per_device(): lax.all_to_all(sent, ('gx', 'gy'), split_axis=0, concat_axis=0, tiled=True)  6.08 us
    pallas_call x1, Pallas kernels, per_device(): pl.pallas_call(lambda *refs: bucket_kernel(*refs, devices=devices, cap=ca...  4.8 us
    ppermute x4, waiting for transfers between devices, exchanged(): got.append(lax.ppermute(jnp.where(lower, last, first), axis, pairs))  3.03 us
    unnamed x8, local copies, waits for them, and re-layouts  1.37 us
    add x2, other arithmetic, per_device(): return (gas_density + smooth[0], gas_rest + smooth[1:])  1.25 us
  transfers between devices with their start and end apart: 5, of which 2 were waited for; matrix products, arithmetic and copies ran while one was open for 0% of the time, Pallas kernels for 0%

profile of v2, /device:TPU:6, one launch (start us, length us, event | category | flops | bytes accessed | tf_op | source)
XLA Modules:
  0.0 49.3 jit_solution(14047286168451430533)
XLA Ops:
  0.6 4.8 %bucket.1 = f32[64,8,256]{2,1,0:T(8,128)} custom-call(f32[16,4096]{1,0:T(8,128)} %refs_0_.1, s32[1,4096]{1,0:T(1,128)} %bitcast.9, s32[1,4096]{1,0:T(1,128)} %bitcast.10, s32[1,4096]{1,0:T(1,128)} %bitcast.11, f32[8,16]{1,0:T(8,128)} %tab_ref.1), custom_call_target="tpu_custom_call" | custom-call | tf_op jit(solution)/shard_map/bucket/pallas_call | solution.py:183
  5.4 6.1 %all-to-all-start = ((f32[64,8,256]{2,1,0:T(8,128)}), f32[64,8,256]{2,1,0:T(8,128)S(1)}, u32[]{:S(2)}, u32[]{:S(2)}) async-start(f32[64,8,256]{2,1,0:T(8,128)} %bucket.1), calls=%async_computation | async-start | bytes 1048576 | tf_op jit(solution)/shard_map/all_to_all | solution.py:197
  11.5 14.7 %all-to-all-done = f32[64,8,256]{2,1,0:T(8,128)S(1)} async-done(((f32[64,8,256]{2,1,0:T(8,128)}), f32[64,8,256]{2,1,0:T(8,128)S(1)}, u32[]{:S(2)}, u32[]{:S(2)}) %all-to-all-start) | async-done | bytes 524320 | tf_op jit(solution)/shard_map/all_to_all | solution.py:197
  26.2 0.0 copy-start
  26.2 0.8 %copy-done = f32[64,8,256]{2,1,0:T(8,128)} copy-done((f32[64,8,256]{2,1,0:T(8,128)}, f32[64,8,256]{2,1,0:T(8,128)S(1)}, u32[]{:S(2)}) %copy-start) | copy-done | bytes 524312
  27.0 8.9 %owner.1 = f32[5,32,128]{2,1,0:T(8,128)} custom-call(f32[512,256]{1,0:T(8,128)} %bitcast.8, f32[8,16]{1,0:T(8,128)} %tab_ref.1, f32[32,128]{1,0:T(8,128)} %rho_ref.1, f32[4,32,128]{2,1,0:T(8,128)} %rest_ref.1), custom_call_target="tpu_custom_call" | custom-call | tf_op jit(solution)/shard_map/owner/pallas_call | solution.py:201
  35.9 0.0 copy-start.1
  35.9 1.1 %slice_select_fusion.1 = (f32[5,32,1]{2,1,0:T(8,128)S(1)}, f32[5,32,1]{2,1,0:T(8,128)S(1)}) fusion(f32[5,32,128]{2,1,0:T(8,128)} %owner.1, pred[]{:T(512)S(6)} %eq.10, pred[]{:T(512)S(6)} %not.7), kind=kLoop, calls=%fused_computation.10 | loop fusion | flops 320 | bytes 2562 | tf_op jit(solution)/shard_map/jit(_where)/select_n | solution.py:167
  37.0 0.1 collective-permute-start.2
  37.1 2.9 %collective-permute-start.3 = (f32[5,32,1]{2,1,0:T(8,128)S(1)}, f32[5,32,1]{2,1,0:T(8,128)S(1)}, u32[]{:S(2)}, u32[]{:S(2)}) collective-permute-start(f32[5,32,1]{2,1,0:T(8,128)S(1)} %get-tuple-element.7), channel_id=1, source_target_pairs={{1,2},{2,1},{5,6},{6,5},{9,10},{10,9},{13,14},{14,13},{17,18},{18,... | collective-permute-start | bytes 1928 | tf_op jit(solution)/shard_map/ppermute | solution.py:167
  40.0 0.0 copy-done.1
  40.0 0.9 %collective-permute-start = (f32[5,1,128]{2,1,0:T(1,128)S(1)}, f32[5,1,128]{2,1,0:T(1,128)S(1)}, u32[]{:S(2)}, u32[]{:S(2)}) collective-permute-start(f32[5,1,128]{2,1,0:T(1,128)S(1)} %get-tuple-element.4), channel_id=1, source_target_pairs={{0,4},{8,12},{16,20},{24,28},{4,0},{12,8},{20,16},{28,24},{1,5},{9... | collective-permute-start | bytes 7688 | tf_op jit(solution)/shard_map/ppermute | solution.py:167
  40.9 3.3 %collective-permute-start.1 = (f32[5,1,128]{2,1,0:T(1,128)S(1)}, f32[5,1,128]{2,1,0:T(1,128)S(1)}, u32[]{:S(2)}, u32[]{:S(2)}) collective-permute-start(f32[5,1,128]{2,1,0:T(1,128)S(1)} %get-tuple-element.5), channel_id=1, source_target_pairs={{4,8},{12,16},{20,24},{8,4},{16,12},{24,20},{5,9},{13,17},{21,25},... | collective-permute-start | bytes 7688 | tf_op jit(solution)/shard_map/ppermute | solution.py:167
  44.2 0.0 collective-permute-done.2
  44.2 0.0 collective-permute-done.3
  44.3 0.0 collective-permute-done
  44.3 3.0 %collective-permute-done.1 = f32[5,1,128]{2,1,0:T(1,128)S(1)} collective-permute-done((f32[5,1,128]{2,1,0:T(1,128)S(1)}, f32[5,1,128]{2,1,0:T(1,128)S(1)}, u32[]{:S(2)}, u32[]{:S(2)}) %collective-permute-start.1) | collective-permute-done | bytes 2592 | tf_op jit(solution)/shard_map/ppermute | solution.py:167
  47.3 0.0 copy-start.3
  47.3 0.0 copy-start.2
  47.3 0.1 fusion.2
  47.5 0.6 %copy-done.3 = f32[32,128]{1,0:T(8,128)S(1)} copy-done((f32[32,128]{1,0:T(8,128)S(1)}, f32[32,128]{1,0:T(8,128)}, u32[]{:S(2)}) %copy-start.3) | copy-done | bytes 16408
  48.0 0.6 %fusion.5 = f32[32,128]{1,0:T(8,128)} fusion(f32[32,128]{1,0:T(8,128)S(1)} %copy-done.3, f32[5,32,128]{2,1,0:T(8,128)S(1)} %fusion.2), kind=kLoop, calls=%fused_computation.15 | loop fusion | flops 4096 | bytes 49152 | tf_op jit(solution)/shard_map/add | solution.py:221
  48.6 0.0 copy-done.2
  48.6 0.6 %slice_add_fusion = f32[4,32,128]{2,1,0:T(8,128)} fusion(f32[4,32,128]{2,1,0:T(8,128)S(1)} %copy-done.2, f32[5,32,128]{2,1,0:T(8,128)S(1)} %fusion.2), kind=kLoop, calls=%fused_computation.11 | loop fusion | flops 16384 | bytes 196608 | tf_op jit(solution)/shard_map/add | solution.py:221
  (3 shorter events, 0.0 us)
Async XLA Ops:
  5.4 20.8 %all-to-all-start = ((f32[64,8,256]{2,1,0:T(8,128)}), f32[64,8,256]{2,1,0:T(8,128)S(1)}, u32[]{:S(2)}, u32[]{:S(2)}) async-start(f32[64,8,256]{2,1,0:T(8,128)} %bucket.1), calls=%async_computation | async-start | bytes 1048576 | tf_op jit(solution)/shard_map/all_to_all | solution.py:197
  26.2 0.8 %copy-start = (f32[64,8,256]{2,1,0:T(8,128)}, f32[64,8,256]{2,1,0:T(8,128)S(1)}, u32[]{:S(2)}) copy-start(f32[64,8,256]{2,1,0:T(8,128)S(1)} %all-to-all-done) | copy-start | bytes 1572868
  35.9 4.1 %copy-start.1 = (f32[5,32,128]{2,1,0:T(8,128)S(1)}, f32[5,32,128]{2,1,0:T(8,128)}, u32[]{:S(2)}) copy-start(f32[5,32,128]{2,1,0:T(8,128)} %owner.1) | copy-start | bytes 245764
  37.0 7.2 %collective-permute-start.2 = (f32[5,32,1]{2,1,0:T(8,128)S(1)}, f32[5,32,1]{2,1,0:T(8,128)S(1)}, u32[]{:S(2)}, u32[]{:S(2)}) collective-permute-start(f32[5,32,1]{2,1,0:T(8,128)S(1)} %get-tuple-element.6), channel_id=1, source_target_pairs={{0,1},{2,3},{1,0},{3,2},{4,5},{6,7},{5,4},{7,6},{8,9},{10,11},{9,8... | collective-permute-start | bytes 1928 | tf_op jit(solution)/shard_map/ppermute | solution.py:167
  37.1 7.1 %collective-permute-start.3 = (f32[5,32,1]{2,1,0:T(8,128)S(1)}, f32[5,32,1]{2,1,0:T(8,128)S(1)}, u32[]{:S(2)}, u32[]{:S(2)}) collective-permute-start(f32[5,32,1]{2,1,0:T(8,128)S(1)} %get-tuple-element.7), channel_id=1, source_target_pairs={{1,2},{2,1},{5,6},{6,5},{9,10},{10,9},{13,14},{14,13},{17,18},{18,... | collective-permute-start | bytes 1928 | tf_op jit(solution)/shard_map/ppermute | solution.py:167
  40.0 4.2 %collective-permute-start = (f32[5,1,128]{2,1,0:T(1,128)S(1)}, f32[5,1,128]{2,1,0:T(1,128)S(1)}, u32[]{:S(2)}, u32[]{:S(2)}) collective-permute-start(f32[5,1,128]{2,1,0:T(1,128)S(1)} %get-tuple-element.4), channel_id=1, source_target_pairs={{0,4},{8,12},{16,20},{24,28},{4,0},{12,8},{20,16},{28,24},{1,5},{9... | collective-permute-start | bytes 7688 | tf_op jit(solution)/shard_map/ppermute | solution.py:167
  40.9 6.4 %collective-permute-start.1 = (f32[5,1,128]{2,1,0:T(1,128)S(1)}, f32[5,1,128]{2,1,0:T(1,128)S(1)}, u32[]{:S(2)}, u32[]{:S(2)}) collective-permute-start(f32[5,1,128]{2,1,0:T(1,128)S(1)} %get-tuple-element.5), channel_id=1, source_target_pairs={{4,8},{12,16},{20,24},{8,4},{16,12},{24,20},{5,9},{13,17},{21,25},... | collective-permute-start | bytes 7688 | tf_op jit(solution)/shard_map/ppermute | solution.py:167
  47.3 0.7 %copy-start.3 = (f32[32,128]{1,0:T(8,128)S(1)}, f32[32,128]{1,0:T(8,128)}, u32[]{:S(2)}) copy-start(f32[32,128]{1,0:T(8,128)} %rho_ref.1) | copy-start | bytes 49156
  47.3 1.3 %copy-start.2 = (f32[4,32,128]{2,1,0:T(8,128)S(1)}, f32[4,32,128]{2,1,0:T(8,128)}, u32[]{:S(2)}) copy-start(f32[4,32,128]{2,1,0:T(8,128)} %rest_ref.1) | copy-start | bytes 196612

commit v3 on v2

--- a/solution.py
+++ b/solution.py
@@ -98,7 +98,7 @@
     groups = x_ref.shape[0] // (rows * VALUES)
     y_shift = shift_of(LANES)
 
-    def group(g, _):
+    def group(g, b):
         base = g * (rows * VALUES)
         mass, q1, q2, q3, q4, total, cls, cell = [
             jnp.concatenate(
@@ -113,7 +113,7 @@
         masks = []
         for r in range(rows):
             y_hot = hot(LANES, cell_y[r : r + 1])
-            y_ref[:, r * LANES : (r + 1) * LANES] = y_hot
+            y_ref[b, :, r * LANES : (r + 1) * LANES] = y_hot
             found = jnp.dot(g_ref[...], y_hot, preferred_element_type=F32)
             mask = lax.broadcasted_iota(I32, (xs, LANES), 0) == cell_x[r : r + 1]
             masks.append(mask)
@@ -144,12 +144,17 @@
             for r in range(rows):
                 line = jnp.where(masks[r], source[c][r : r + 1], 0.0)
                 top, low = split2(line)
-                a_ref[c * xs : (c + 1) * xs, r * LANES : (r + 1) * LANES] = top
-                a_ref[(5 + c) * xs : (6 + c) * xs, r * LANES : (r + 1) * LANES] = low
-        acc_ref[...] += lax.dot_general(a_ref[...], y_ref[...], NT, preferred_element_type=F32)
+                a_ref[b, c * xs : (c + 1) * xs, r * LANES : (r + 1) * LANES] = top
+                a_ref[b, (5 + c) * xs : (6 + c) * xs, r * LANES : (r + 1) * LANES] = low
+        acc_ref[...] += lax.dot_general(a_ref[b], y_ref[b], NT, preferred_element_type=F32)
+
+    def couple(i, _):
+        group(2 * i, 0)
+        group(2 * i + 1, 1)
         return 0
 
-    lax.fori_loop(0, groups, group, 0)
+    assert groups % 2 == 0
+    lax.fori_loop(0, groups // 2, couple, 0)
     for c in range(5):
         both = acc_ref[c * xs : (c + 1) * xs, :] + acc_ref[(5 + c) * xs : (6 + c) * xs, :]
         for f in range(fold):
@@ -205,8 +210,8 @@
         out_specs=vmem,
         scratch_shapes=[
             pltpu.VMEM((8 * xs, LANES), BF16),
-            pltpu.VMEM((LANES, 8 * LANES), BF16),
-            pltpu.VMEM((10 * xs, 8 * LANES), BF16),
+            pltpu.VMEM((2, LANES, 8 * LANES), BF16),
+            pltpu.VMEM((2, 10 * xs, 8 * LANES), BF16),
             pltpu.VMEM((10 * xs, LANES), F32),
             pltpu.VMEM((2, slots // LANES * VALUES, LANES // 2), F32),
         ],

time: 49.6 us -> 50.6 us (1.020)
  Pallas kernels: 13.7 us -> 14.6 us
    pallas_call x1, Pallas kernels: 8.86 us -> 9.76 us  [per_device(): pl.pallas_call(owner_kernel, out_shape=jax.ShapeDtypeStruct((5, slab_x, s...]
where the time goes in v3:
time: 50.6 us; the launch traced here: 50.2 us
  waiting for transfers between devices  17.7 us (35%)
  Pallas kernels  14.6 us (29%)
  starting transfers between devices  13.2 us (26%)
  other arithmetic  2.53 us (5%)
  local copies, waits for them, and re-layouts  1.37 us (3%)
  between operations  0.76 us (2%)
    all_to_all x1, waiting for transfers between devices, per_device(): lax.all_to_all(sent, ('gx', 'gy'), split_axis=0, concat_axis=0, tiled=True)  14.7 us
    pallas_call x1, Pallas kernels, per_device(): pl.pallas_call(owner_kernel, out_shape=jax.ShapeDtypeStruct((5, slab_x, s...  9.76 us
    ppermute x4, starting transfers between devices, exchanged(): got.append(lax.ppermute(jnp.where(lower, last, first), axis, pairs))  7.15 us
    all_to_all x1, starting transfers between devices, per_device(): lax.all_to_all(sent, ('gx', 'gy'), split_axis=0, concat_axis=0, tiled=True)  6.08 us
    pallas_call x1, Pallas kernels, per_device(): pl.pallas_call(lambda *refs: bucket_kernel(*refs, devices=devices, cap=ca...  4.8 us
    ppermute x4, waiting for transfers between devices, exchanged(): got.append(lax.ppermute(jnp.where(lower, last, first), axis, pairs))  3.03 us
    unnamed x8, local copies, waits for them, and re-layouts  1.37 us
    add x2, other arithmetic, per_device(): return (gas_density + smooth[0], gas_rest + smooth[1:])  1.25 us
  transfers between devices with their start and end apart: 5, of which 2 were waited for; matrix products, arithmetic and copies ran while one was open for 0% of the time, Pallas kernels for 0%

profile of v3, /device:TPU:6, one launch (start us, length us, event | category | flops | bytes accessed | tf_op | source)
XLA Modules:
  0.0 50.2 jit_solution(7391776405708628230)
XLA Ops:
  0.6 4.8 %bucket.1 = f32[64,8,256]{2,1,0:T(8,128)} custom-call(f32[16,4096]{1,0:T(8,128)} %refs_0_.1, s32[1,4096]{1,0:T(1,128)} %bitcast.9, s32[1,4096]{1,0:T(1,128)} %bitcast.10, s32[1,4096]{1,0:T(1,128)} %bitcast.11, f32[8,16]{1,0:T(8,128)} %tab_ref.1), custom_call_target="tpu_custom_call" | custom-call | tf_op jit(solution)/shard_map/bucket/pallas_call | solution.py:188
  5.4 6.1 %all-to-all-start = ((f32[64,8,256]{2,1,0:T(8,128)}), f32[64,8,256]{2,1,0:T(8,128)S(1)}, u32[]{:S(2)}, u32[]{:S(2)}) async-start(f32[64,8,256]{2,1,0:T(8,128)} %bucket.1), calls=%async_computation | async-start | bytes 1048576 | tf_op jit(solution)/shard_map/all_to_all | solution.py:202
  11.5 14.7 %all-to-all-done = f32[64,8,256]{2,1,0:T(8,128)S(1)} async-done(((f32[64,8,256]{2,1,0:T(8,128)}), f32[64,8,256]{2,1,0:T(8,128)S(1)}, u32[]{:S(2)}, u32[]{:S(2)}) %all-to-all-start) | async-done | bytes 524320 | tf_op jit(solution)/shard_map/all_to_all | solution.py:202
  26.2 0.0 copy-start
  26.2 0.8 %copy-done = f32[64,8,256]{2,1,0:T(8,128)} copy-done((f32[64,8,256]{2,1,0:T(8,128)}, f32[64,8,256]{2,1,0:T(8,128)S(1)}, u32[]{:S(2)}) %copy-start) | copy-done | bytes 524312
  27.0 9.8 %owner.1 = f32[5,32,128]{2,1,0:T(8,128)} custom-call(f32[512,256]{1,0:T(8,128)} %bitcast.8, f32[8,16]{1,0:T(8,128)} %tab_ref.1, f32[32,128]{1,0:T(8,128)} %rho_ref.1, f32[4,32,128]{2,1,0:T(8,128)} %rest_ref.1), custom_call_target="tpu_custom_call" | custom-call | tf_op jit(solution)/shard_map/owner/pallas_call | solution.py:206
  36.8 0.0 copy-start.1
  36.8 1.1 %slice_select_fusion.1 = (f32[5,32,1]{2,1,0:T(8,128)S(1)}, f32[5,32,1]{2,1,0:T(8,128)S(1)}) fusion(f32[5,32,128]{2,1,0:T(8,128)} %owner.1, pred[]{:T(512)S(6)} %eq.10, pred[]{:T(512)S(6)} %not.7), kind=kLoop, calls=%fused_computation.10 | loop fusion | flops 320 | bytes 2562 | tf_op jit(solution)/shard_map/jit(_where)/select_n | solution.py:172
  37.9 0.1 collective-permute-start.2
  38.0 2.9 %collective-permute-start.3 = (f32[5,32,1]{2,1,0:T(8,128)S(1)}, f32[5,32,1]{2,1,0:T(8,128)S(1)}, u32[]{:S(2)}, u32[]{:S(2)}) collective-permute-start(f32[5,32,1]{2,1,0:T(8,128)S(1)} %get-tuple-element.7), channel_id=1, source_target_pairs={{1,2},{2,1},{5,6},{6,5},{9,10},{10,9},{13,14},{14,13},{17,18},{18,... | collective-permute-start | bytes 1928 | tf_op jit(solution)/shard_map/ppermute | solution.py:172
  40.9 0.0 copy-done.1
  40.9 0.9 %collective-permute-start = (f32[5,1,128]{2,1,0:T(1,128)S(1)}, f32[5,1,128]{2,1,0:T(1,128)S(1)}, u32[]{:S(2)}, u32[]{:S(2)}) collective-permute-start(f32[5,1,128]{2,1,0:T(1,128)S(1)} %get-tuple-element.4), channel_id=1, source_target_pairs={{0,4},{8,12},{16,20},{24,28},{4,0},{12,8},{20,16},{28,24},{1,5},{9... | collective-permute-start | bytes 7688 | tf_op jit(solution)/shard_map/ppermute | solution.py:172
  41.8 3.3 %collective-permute-start.1 = (f32[5,1,128]{2,1,0:T(1,128)S(1)}, f32[5,1,128]{2,1,0:T(1,128)S(1)}, u32[]{:S(2)}, u32[]{:S(2)}) collective-permute-start(f32[5,1,128]{2,1,0:T(1,128)S(1)} %get-tuple-element.5), channel_id=1, source_target_pairs={{4,8},{12,16},{20,24},{8,4},{16,12},{24,20},{5,9},{13,17},{21,25},... | collective-permute-start | bytes 7688 | tf_op jit(solution)/shard_map/ppermute | solution.py:172
  45.1 0.0 collective-permute-done.2
  45.1 0.0 collective-permute-done.3
  45.2 0.0 collective-permute-done
  45.2 3.0 %collective-permute-done.1 = f32[5,1,128]{2,1,0:T(1,128)S(1)} collective-permute-done((f32[5,1,128]{2,1,0:T(1,128)S(1)}, f32[5,1,128]{2,1,0:T(1,128)S(1)}, u32[]{:S(2)}, u32[]{:S(2)}) %collective-permute-start.1) | collective-permute-done | bytes 2592 | tf_op jit(solution)/shard_map/ppermute | solution.py:172
  48.2 0.0 copy-start.3
  48.2 0.0 copy-start.2
  48.2 0.1 fusion.2
  48.4 0.6 %copy-done.3 = f32[32,128]{1,0:T(8,128)S(1)} copy-done((f32[32,128]{1,0:T(8,128)S(1)}, f32[32,128]{1,0:T(8,128)}, u32[]{:S(2)}) %copy-start.3) | copy-done | bytes 16408
  48.9 0.6 %fusion.5 = f32[32,128]{1,0:T(8,128)} fusion(f32[32,128]{1,0:T(8,128)S(1)} %copy-done.3, f32[5,32,128]{2,1,0:T(8,128)S(1)} %fusion.2), kind=kLoop, calls=%fused_computation.15 | loop fusion | flops 4096 | bytes 49152 | tf_op jit(solution)/shard_map/add | solution.py:226
  49.5 0.0 copy-done.2
  49.5 0.6 %slice_add_fusion = f32[4,32,128]{2,1,0:T(8,128)} fusion(f32[4,32,128]{2,1,0:T(8,128)S(1)} %copy-done.2, f32[5,32,128]{2,1,0:T(8,128)S(1)} %fusion.2), kind=kLoop, calls=%fused_computation.11 | loop fusion | flops 16384 | bytes 196608 | tf_op jit(solution)/shard_map/add | solution.py:226
  (3 shorter events, 0.0 us)
Async XLA Ops:
  5.4 20.8 %all-to-all-start = ((f32[64,8,256]{2,1,0:T(8,128)}), f32[64,8,256]{2,1,0:T(8,128)S(1)}, u32[]{:S(2)}, u32[]{:S(2)}) async-start(f32[64,8,256]{2,1,0:T(8,128)} %bucket.1), calls=%async_computation | async-start | bytes 1048576 | tf_op jit(solution)/shard_map/all_to_all | solution.py:202
  26.2 0.8 %copy-start = (f32[64,8,256]{2,1,0:T(8,128)}, f32[64,8,256]{2,1,0:T(8,128)S(1)}, u32[]{:S(2)}) copy-start(f32[64,8,256]{2,1,0:T(8,128)S(1)} %all-to-all-done) | copy-start | bytes 1572868
  36.8 4.1 %copy-start.1 = (f32[5,32,128]{2,1,0:T(8,128)S(1)}, f32[5,32,128]{2,1,0:T(8,128)}, u32[]{:S(2)}) copy-start(f32[5,32,128]{2,1,0:T(8,128)} %owner.1) | copy-start | bytes 245764
  37.9 7.2 %collective-permute-start.2 = (f32[5,32,1]{2,1,0:T(8,128)S(1)}, f32[5,32,1]{2,1,0:T(8,128)S(1)}, u32[]{:S(2)}, u32[]{:S(2)}) collective-permute-start(f32[5,32,1]{2,1,0:T(8,128)S(1)} %get-tuple-element.6), channel_id=1, source_target_pairs={{0,1},{2,3},{1,0},{3,2},{4,5},{6,7},{5,4},{7,6},{8,9},{10,11},{9,8... | collective-permute-start | bytes 1928 | tf_op jit(solution)/shard_map/ppermute | solution.py:172
  38.0 7.1 %collective-permute-start.3 = (f32[5,32,1]{2,1,0:T(8,128)S(1)}, f32[5,32,1]{2,1,0:T(8,128)S(1)}, u32[]{:S(2)}, u32[]{:S(2)}) collective-permute-start(f32[5,32,1]{2,1,0:T(8,128)S(1)} %get-tuple-element.7), channel_id=1, source_target_pairs={{1,2},{2,1},{5,6},{6,5},{9,10},{10,9},{13,14},{14,13},{17,18},{18,... | collective-permute-start | bytes 1928 | tf_op jit(solution)/shard_map/ppermute | solution.py:172
  40.9 4.2 %collective-permute-start = (f32[5,1,128]{2,1,0:T(1,128)S(1)}, f32[5,1,128]{2,1,0:T(1,128)S(1)}, u32[]{:S(2)}, u32[]{:S(2)}) collective-permute-start(f32[5,1,128]{2,1,0:T(1,128)S(1)} %get-tuple-element.4), channel_id=1, source_target_pairs={{0,4},{8,12},{16,20},{24,28},{4,0},{12,8},{20,16},{28,24},{1,5},{9... | collective-permute-start | bytes 7688 | tf_op jit(solution)/shard_map/ppermute | solution.py:172
  41.8 6.4 %collective-permute-start.1 = (f32[5,1,128]{2,1,0:T(1,128)S(1)}, f32[5,1,128]{2,1,0:T(1,128)S(1)}, u32[]{:S(2)}, u32[]{:S(2)}) collective-permute-start(f32[5,1,128]{2,1,0:T(1,128)S(1)} %get-tuple-element.5), channel_id=1, source_target_pairs={{4,8},{12,16},{20,24},{8,4},{16,12},{24,20},{5,9},{13,17},{21,25},... | collective-permute-start | bytes 7688 | tf_op jit(solution)/shard_map/ppermute | solution.py:172
  48.2 0.7 %copy-start.3 = (f32[32,128]{1,0:T(8,128)S(1)}, f32[32,128]{1,0:T(8,128)}, u32[]{:S(2)}) copy-start(f32[32,128]{1,0:T(8,128)} %rho_ref.1) | copy-start | bytes 49156
  48.2 1.3 %copy-start.2 = (f32[4,32,128]{2,1,0:T(8,128)S(1)}, f32[4,32,128]{2,1,0:T(8,128)}, u32[]{:S(2)}) copy-start(f32[4,32,128]{2,1,0:T(8,128)} %rest_ref.1) | copy-start | bytes 196612
